TPU v7x, 256 devices: a whole 4x4x8 slice. The times are simulated.
256 devices in a mesh: section: 2 (over core), rep: 16 (over z_lo, y), tp: 8 (over z_hi, x).
Axes of the slice: x: 4, y: 4, z: 8 (z_hi: 2, z_lo: 4; z = z_hi * 4 + z_lo), core: 2. Of those that a mesh axis runs over, the one named last changes fastest.
Arguments:
- tokens: bfloat16 [32768, 8192], P(('section', 'rep'), 'tp'), may hold values from -6 to 6
- norm_gain: bfloat16 [8192], P('tp'), may hold values from 0.099609375 to 1.8984375
- kv_weight: bfloat16 [8192, 2048], P('tp'), may hold values from -0.0625 to 0.0625
- page_dest: int32 [2048, 1], P(('section', 'rep')), may hold values from 0 to 31; in each aligned block of 64 rows (0 to 63, 64 to 127, ...) at most 4 rows name the same one
- page_row: int32 [2048], P(('section', 'rep')), may hold values from 0 to 7
- queries: bfloat16 [256, 8192], P(('section', 'rep'), 'tp'), may hold values from -250 to 250
- kv_pool: bfloat16 [1024, 16, 2048], P(('section', 'rep'), None, 'tp'), may hold values from -9 to 9
- block_table: int32 [256, 4], P(('section', 'rep')), may hold values from 0 to 31, as said below
- ctx_len: int32 [256], P(('section', 'rep')), may hold values from 2 to 64
- new_kv: bfloat16 [256, 2048], P(('section', 'rep'), 'tp'), may hold values from -6 to 6
Outputs:
- attended: bfloat16 [256, 8192], P(('section', 'rep'), 'tp')
Inputs may be any that keep to these rules, and one draw needn't show every extreme that they name: `page_dest`: at most 4 of the new pages of one owner go to the same owner. `block_table`: the rows of one owner name each of its 32 local pages exactly once.
All inputs are finite; a program needn't handle non-finite values.
Results may differ from a plain program's by a relative error of at most 0.019.
Values may be sent and summed in bfloat16 or wider, within the bound.
No kernel may reach another device: no remote copies, remote signals or barrier semaphores. Data moves between devices by JAX's collectives and lax.ppermute only.
A program may use at most 64 MiB of HBM per device.

v0:
```python
import jax
import jax.numpy as jnp
from jax import lax
from jax.experimental import pallas as pl
from jax.experimental.pallas import tpu as pltpu
from jax.sharding import Mesh
from jax.sharding import PartitionSpec as P

HD = 128
PAGE = 16
SLOT = 4
EPS = 1e-06
OWN = ("section", "rep")
NEAR = ((0, 1), (1, 0), (2, 3), (3, 2))
FAR = ((0, 3), (3, 0), (1, 2), (2, 1))
SWAP = ((0, 1), (1, 0))
F32 = jnp.float32
BF = jnp.bfloat16


def nt(a, b):
    return lax.dot_general(a, b, (((1,), (1,)), ((), ())), preferred_element_type=F32)


def blocks_for(names):
    x = lax.axis_index("tp_1")
    near, far = x ^ 1, 3 - x
    heads = {
        "a_send": (3 - near, near),
        "b_send": (4 + (far ^ 1), 4 + far),
        "a_keep": (3 - x, x),
        "b_keep": (4 + near, 4 + x),
    }
    return [2 * h + kv for name, kv in names for h in heads[name]]


def load_all(names, tok, w, tokv, wv, tsem, wsem):
    rows = tokv.shape[0] // tsem.shape[0]
    fetch = [
        pltpu.make_async_copy(
            w.at[:, pl.ds(pl.multiple_of(c * HD, HD), HD)], wv.at[:, k * HD : (k + 1) * HD], wsem.at[k]
        )
        for k, c in enumerate(blocks_for(names))
    ]
    chunks = [
        pltpu.make_async_copy(
            tok.at[m * rows : (m + 1) * rows, :], tokv.at[m * rows : (m + 1) * rows, :], tsem.at[m]
        )
        for m in range(tsem.shape[0])
    ]
    for c in chunks[:1] + fetch[:4] + chunks[1:] + fetch[4:]:
        c.start()
    return fetch, chunks, rows


NAMES = (
    ("a_send", 0), ("b_send", 0), ("a_send", 1), ("b_send", 1),
    ("a_keep", 0), ("b_keep", 0), ("a_keep", 1), ("b_keep", 1),
)


def project_kernel(tok, gain, w, *refs):
    outs = refs[:16]
    tokv, wv, obuf, ssq, gainv, tsem, wsem, osem, gsem = refs[16:]
    early = pltpu.make_async_copy(gain, gainv, gsem)
    early.start()
    fetch, chunks, rows = load_all(NAMES, tok, w, tokv, wv, tsem, wsem)
    n, d = tokv.shape
    early.wait()
    g = gainv[...].astype(F32).reshape(1, -1)
    done = []

    def ship(k):
        c = pltpu.make_async_copy(obuf.at[k, 0 : outs[k].shape[0], :], outs[k], osem.at[k])
        c.start()
        done.append(c)

    for k in range(0, 16, 4):
        for m, c in enumerate(chunks):
            at = slice(m * rows, (m + 1) * rows)
            if k == 0:
                c.wait()
                x = tokv[at, :].astype(F32)
                tokv[at, :] = (x * g).astype(BF)
                sq = x * x
                part = sum(sq[:, i : i + HD] for i in range(0, d, HD))
                ssq[:, at] = nt(jnp.ones((8, HD), BF), part.astype(BF))
            if m == 0:
                for f in fetch[k : k + 4]:
                    f.wait()
            r = jnp.dot(tokv[at, :], wv[:, k * HD : (k + 4) * HD], preferred_element_type=F32).astype(BF)
            for i in range(4):
                if k < 8:
                    obuf[k + i, at, :] = r[:, i * HD : (i + 1) * HD]
                else:
                    outs[k + i][at, :] = r[:, i * HD : (i + 1) * HD]
        if k == 0:
            parts = [ssq[0:1, i * HD : (i + 1) * HD] for i in range(n // HD)]
            tile = jnp.concatenate(parts + [jnp.zeros((16 - n // HD, HD), F32)], axis=0).astype(BF)
            for i in range(4):
                obuf[i, n : n + 16, :] = tile
                outs[8 + i][n : n + 16, :] = tile
        if k < 8:
            for i in range(4):
                ship(k + i)
    for c in done:
        c.wait()


VM = 48 << 20


def projection(kernel, count, chunks, tokens, gain, weight, extra, shapes, scratch, outs, sems):
    n, d = tokens.shape
    hbm = pl.BlockSpec(memory_space=pltpu.HBM)
    vmem = pl.BlockSpec(memory_space=pltpu.VMEM)
    return pl.pallas_call(
        kernel,
        in_specs=[hbm, hbm, hbm] + [vmem for _ in extra],
        out_specs=outs,
        scratch_shapes=[pltpu.VMEM((n, d), BF), pltpu.VMEM((d, count * HD), BF)]
        + scratch
        + [pltpu.SemaphoreType.DMA((chunks,)), pltpu.SemaphoreType.DMA((count,))]
        + sems,
        out_shape=[jax.ShapeDtypeStruct(s, BF) for s in shapes],
        compiler_params=pltpu.CompilerParams(vmem_limit_bytes=VM),
    )(tokens, gain, weight, *extra)


def pair_kernel(a0, a1, b0, b1, oa, ob):
    oa[...] = a0[...] + a1[...]
    ob[...] = b0[...] + b1[...]


def pair_sum(a0, a1, b0, b1):
    return pl.pallas_call(
        pair_kernel, out_shape=[jax.ShapeDtypeStruct(a0.shape, BF)] * 2, compiler_params=small()
    )(a0, a1, b0, b1)


def own_kernel(a0, a1, a2, b0, b1, b2, give, keep):
    first = (lax.axis_index("tp_0") == 0).astype(jnp.int32)
    a = (a0[...].astype(F32) + a1[...].astype(F32) + a2[...].astype(F32)).astype(BF)
    b = (b0[...].astype(F32) + b1[...].astype(F32) + b2[...].astype(F32)).astype(BF)

    @pl.when(first == 1)
    def _():
        give[...] = b
        keep[...] = a

    @pl.when(first == 0)
    def _():
        give[...] = a
        keep[...] = b


def own_sum(*parts):
    return pl.pallas_call(
        own_kernel,
        out_shape=[jax.ShapeDtypeStruct(parts[0].shape, BF)] * 2,
        compiler_params=small(8),
    )(*parts)


def split3(x):
    hi = x.astype(BF)
    left = x - hi.astype(F32)
    mid = left.astype(BF)
    low = (left - mid.astype(F32)).astype(BF)
    return hi, mid, low


def page_group(x, op):
    lane = lax.broadcasted_iota(jnp.int32, x.shape, 1)
    n = x.shape[1]
    for k in (1, 2, 4, 8):
        other = jnp.where((lane & k) == 0, pltpu.roll(x, n - k, 1), pltpu.roll(x, k, 1))
        x = op(x, other)
    return x


def prepare_kernel(qown, qother, dest, row, mine, qpage, psel, wide, tags):
    pages = dest.shape[1]
    n = wide.shape[1]
    per_owner = 8
    dest_f, row_f = dest[...].astype(F32), row[...].astype(F32)
    p0 = lax.broadcasted_iota(jnp.int32, (pages, pages), 0)
    p1 = lax.broadcasted_iota(jnp.int32, (pages, pages), 1)
    column = lambda v: jnp.sum(jnp.where(p0 == p1, v, 0.0), axis=1, keepdims=True)
    dest_c = column(dest_f)
    half = qown.shape[0]
    place = (dest[...] ^ mine[0]).astype(F32)
    where_page = column(place * per_owner + row_f)
    lanes = lax.broadcasted_iota(jnp.int32, (pages, half), 1).astype(F32)
    pick = lambda shift: (lanes + shift == where_page).astype(F32).astype(BF)
    qp = jnp.dot(pick(0.0), qown[...], preferred_element_type=F32) + jnp.dot(
        pick(float(half)), qother[...], preferred_element_type=F32
    )
    bp = PAGE
    for b in range(pages // bp):
        for j in range(8):
            at = (b * 8 + j) * bp
            qpage[at : at + bp, :] = qp[b * bp : (b + 1) * bp, j * HD : (j + 1) * HD].astype(BF)
    rank = jnp.sum(((dest_c == dest_f) & (p0 < p1)).astype(F32), axis=0, keepdims=True)
    place = (dest_f * SLOT + rank) * 2
    slots = psel.shape[1]
    at = lax.broadcasted_iota(jnp.int32, (slots, pages), 0).astype(F32)
    even = (at == place).astype(F32)
    odd = (at == place + 1).astype(F32)
    psel[0] = even.astype(BF)
    psel[1] = odd.astype(BF)
    token = lax.broadcasted_iota(jnp.int32, (pages, n), 1)
    page = lax.broadcasted_iota(jnp.int32, (pages, n), 0)
    head = (token == page * PAGE).astype(F32).astype(BF)
    wide[...] = jnp.dot((even + odd).astype(BF), head, preferred_element_type=F32).astype(BF)
    inside = (token // PAGE == page).astype(F32).astype(BF)
    tag8 = jnp.broadcast_to(row_f + 1.0, (8, pages)).astype(BF)
    tags[...] = jnp.dot(tag8, inside, preferred_element_type=F32)


def small(mib=6):
    return pltpu.CompilerParams(vmem_limit_bytes=mib << 20)


def prepare(qown, qother, dest, row, mine, slots, n):
    pages = dest.shape[1]
    return pl.pallas_call(
        prepare_kernel,
        out_shape=[
            jax.ShapeDtypeStruct((pages * 8, HD), BF),
            jax.ShapeDtypeStruct((2, slots * 2, pages), BF),
            jax.ShapeDtypeStruct((slots * 2, n), BF),
            jax.ShapeDtypeStruct((8, n), F32),
        ],
        in_specs=[pl.BlockSpec(memory_space=pltpu.VMEM)] * 4 + [pl.BlockSpec(memory_space=pltpu.SMEM)],
        compiler_params=small(),
        name="prepare",
    )(qown, qother, dest, row, mine)


def score_kernel(keys0, keys1, qpage, wide, tags, probs, ext, keys):
    n = keys0.shape[0] - 16
    ssum = keys0[n : n + 16, :].astype(F32) + keys1[n : n + 16, :].astype(F32)
    keys[...] = keys0[0:n, :] + keys1[0:n, :]
    block = 256
    bp = block // PAGE
    own = (
        lax.broadcasted_iota(jnp.int32, (bp, block), 1) // PAGE
        == lax.broadcasted_iota(jnp.int32, (bp, block), 0)
    )
    parts = []
    for b in range(n // block):
        q = qpage[b * 8 * bp : (b + 1) * 8 * bp, :]
        s = nt(q, keys[b * block : (b + 1) * block, :]).reshape(8, bp, block)
        parts.append(jnp.sum(jnp.where(own[None], s, 0.0), axis=1))
    total = jnp.concatenate([ssum[i : i + 1, :] for i in range(n // HD)], axis=1)
    scale = lax.rsqrt(total / 8192.0 + EPS)
    s = jnp.concatenate(parts, axis=1) * (scale * HD ** (-0.5))
    top = page_group(s, jnp.maximum)
    e = jnp.exp(s - top)
    mass = page_group(e, jnp.add)
    probs[...] = e / mass * scale
    hi, mid, low = split3(top + jnp.log(mass))
    stack = jnp.concatenate(
        [hi.astype(F32), mid.astype(F32), low.astype(F32), tags[...], jnp.zeros((HD - 32, n), F32)], axis=0
    ).astype(BF)
    ext[...] = nt(wide[...], stack).astype(BF)


def score(keys0, keys1, qpage, wide, tags):
    n = keys0.shape[0] - 16
    return pl.pallas_call(
        score_kernel,
        out_shape=[
            jax.ShapeDtypeStruct((8, n), F32),
            jax.ShapeDtypeStruct((wide.shape[0], HD), BF),
        ],
        scratch_shapes=[pltpu.VMEM((n, HD), BF)],
        compiler_params=small(),
        name="score",
    )(keys0, keys1, qpage, wide, tags)


def value_kernel(values0, values1, probs, ext, psel, out, acc):
    n = values0.shape[0]
    block = 256
    bp = block // PAGE
    own = (
        lax.broadcasted_iota(jnp.int32, (bp, block), 1) // PAGE
        == lax.broadcasted_iota(jnp.int32, (bp, block), 0)
    )
    for b in range(n // block):
        p = probs[:, b * block : (b + 1) * block]
        a = jnp.concatenate(
            [jnp.where(own, p[j : j + 1, :], 0.0) for j in range(8)], axis=0
        ).astype(BF)
        at = slice(b * block, (b + 1) * block)
        o = jnp.dot(a, values0[at, :] + values1[at, :], preferred_element_type=F32)
        for j in range(8):
            acc[b * bp : (b + 1) * bp, j * HD : (j + 1) * HD] = o[j * bp : (j + 1) * bp].astype(BF)
    half = acc.shape[1] // 2
    out[:, :half] = (
        jnp.dot(psel[0], acc[:, :half], preferred_element_type=F32)
        + jnp.dot(psel[1], acc[:, half:], preferred_element_type=F32)
    ).astype(BF)
    out[:, half:] = ext[...]


def value(values0, values1, probs, ext, psel):
    return pl.pallas_call(
        value_kernel,
        out_shape=jax.ShapeDtypeStruct((psel.shape[1], 5 * HD), BF),
        scratch_shapes=[pltpu.VMEM((psel.shape[2], 8 * HD), BF)],
        compiler_params=small(),
        name="value",
    )(values0, values1, probs, ext, psel)


def resident_kernel(queries, pool, table, length, fresh, top_out, mass_out, acc_out):
    rows = queries.shape[0]
    n = pool.shape[0]
    q32 = queries[...].astype(F32)
    q = jnp.concatenate([q32[:, j * HD : (j + 1) * HD] for j in range(8)], axis=0)
    s = nt(q.astype(BF), pool[:, :HD]) * HD ** (-0.5)
    token = lax.broadcasted_iota(jnp.int32, (rows, n), 1)
    valid = jnp.zeros((rows, n), jnp.int32)
    r0 = lax.broadcasted_iota(jnp.int32, (rows, rows), 0)
    r1 = lax.broadcasted_iota(jnp.int32, (rows, rows), 1)
    column = lambda v: jnp.sum(jnp.where(r0 == r1, v, 0), axis=1, keepdims=True)
    long = column(length[...])
    for i in range(table.shape[0]):
        hit = (token // PAGE == column(table[i : i + 1, :])) & (token % PAGE < long - PAGE * i)
        valid = valid + hit.astype(jnp.int32)
    mask = jnp.concatenate([valid] * 8, axis=0) > 0
    own = fresh[...].astype(F32)
    own_k = jnp.concatenate([own[:, :HD]] * 8, axis=0)
    own_v = jnp.concatenate([own[:, HD:]] * 8, axis=0)
    s_own = jnp.sum(q * own_k, axis=1, keepdims=True) * HD ** (-0.5)
    top = jnp.maximum(jnp.max(jnp.where(mask, s, -jnp.inf), axis=1, keepdims=True), s_own)
    e = jnp.where(mask, jnp.exp(s - top), 0.0)
    e_own = jnp.exp(s_own - top)
    top_out[...] = top
    mass_out[...] = jnp.sum(e, axis=1, keepdims=True) + e_own
    acc_out[...] = (
        jnp.dot(e.astype(BF), pool[:, HD:], preferred_element_type=F32) + e_own * own_v
    )


def resident(queries, pool, table, length, fresh):
    n = queries.shape[0] * 8
    return pl.pallas_call(
        resident_kernel,
        out_shape=[
            jax.ShapeDtypeStruct((n, 1), F32),
            jax.ShapeDtypeStruct((n, 1), F32),
            jax.ShapeDtypeStruct((n, HD), F32),
        ],
        compiler_params=small(),
        name="resident",
    )(queries, pool, table, length, fresh)


def merge_kernel(got, top_in, mass_in, acc_in, out):
    rows = out.shape[0]
    slots = got.shape[0]
    ext = got[:, 4 * HD :].astype(F32).T
    lse = ext[0:8] + ext[8:16] + ext[16:24]
    live = ext[24:25] == (lax.broadcasted_iota(jnp.int32, (rows, slots), 0) + 1).astype(F32)
    odd = lax.broadcasted_iota(jnp.int32, (rows, slots), 1) % 2
    for j in range(8):
        mask = live & (odd == j // 4)
        at = slice(j * rows, (j + 1) * rows)
        l = jnp.where(mask, lse[j : j + 1], -jnp.inf)
        top = jnp.maximum(jnp.max(l, axis=1, keepdims=True), top_in[at, :])
        w = jnp.where(mask, jnp.exp(l - top), 0.0)
        keep = jnp.exp(top_in[at, :] - top)
        total = jnp.sum(w, axis=1, keepdims=True) + mass_in[at, :] * keep
        k = j % 4
        o = jnp.dot(w.astype(BF), got[:, k * HD : (k + 1) * HD], preferred_element_type=F32)
        out[:, j * HD : (j + 1) * HD] = ((o + acc_in[at, :] * keep) / total).astype(BF)


def merge(got, top, mass, acc, rows):
    return pl.pallas_call(
        merge_kernel,
        out_shape=jax.ShapeDtypeStruct((rows, 8 * HD), BF),
        compiler_params=small(),
        name="merge",
    )(got, top, mass, acc)


def body(
    tokens,
    norm_gain,
    kv_weight,
    page_dest,
    page_row,
    queries,
    kv_pool,
    block_table,
    ctx_len,
    new_kv,
):
    n, d = tokens.shape
    ext, one = (n + 16, HD), (n, HD)
    gain = norm_gain

    vmem, hbm = pl.BlockSpec(memory_space=pltpu.VMEM), pl.BlockSpec(memory_space=pltpu.HBM)
    (
        kf_a, ko_a, kf_b, ko_b, vf_a, vo_a, vf_b, vo_b,
        kkf_a, kko_a, kkf_b, kko_b, vkf_a, vko_a, vkf_b, vko_b,
    ) = projection(
        project_kernel, 16, 4, tokens, gain, kv_weight, [],
        [ext] * 4 + [one] * 4 + [ext] * 4 + [one] * 4,
        [pltpu.VMEM((8, *ext), BF), pltpu.VMEM((8, n), F32), pltpu.VMEM((d,), BF)], [hbm] * 8 + [vmem] * 8,
        [pltpu.SemaphoreType.DMA((8,)), pltpu.SemaphoreType.DMA],
    )
    k1f_a, k1f_b = lax.ppermute(kf_a, "tp_1", NEAR), lax.ppermute(kf_b, "tp_1", FAR)
    k1o_a, k1o_b = lax.ppermute(ko_a, "tp_1", NEAR), lax.ppermute(ko_b, "tp_1", FAR)
    s_a, s_b = pair_sum(k1f_a, kkf_a, k1f_b, kkf_b)
    k2_a, k2_b = lax.ppermute(s_a, "tp_1", FAR), lax.ppermute(s_b, "tp_1", NEAR)
    v1f_a, v1f_b = lax.ppermute(vf_a, "tp_1", NEAR), lax.ppermute(vf_b, "tp_1", FAR)
    v1o_a, v1o_b = lax.ppermute(vo_a, "tp_1", NEAR), lax.ppermute(vo_b, "tp_1", FAR)
    owners = lax.axis_size(OWN)
    rows = queries.shape[0]
    peers = lax.axis_size("rep")
    spread = jnp.broadcast_to(queries[None], (peers, *queries.shape))
    qown = lax.all_to_all(spread, "rep", 0, 0, tiled=True).reshape(peers * rows, -1)
    qother = lax.ppermute(qown, "section", SWAP)
    s_a, s_b = pair_sum(v1f_a, vkf_a, v1f_b, vkf_b)
    v2_a, v2_b = lax.ppermute(s_a, "tp_1", FAR), lax.ppermute(s_b, "tp_1", NEAR)
    give, keep = own_sum(k1o_a, kko_a, k2_a, k1o_b, kko_b, k2_b)
    keys = (lax.ppermute(give, "tp_0", SWAP), keep)
    give, keep = own_sum(v1o_a, vko_a, v2_a, v1o_b, vko_b, v2_b)
    values = (lax.ppermute(give, "tp_0", SWAP), keep)

    pages = page_row.shape[0]
    mine = lax.axis_index("section").astype(jnp.int32).reshape(1) * peers
    qpage, psel, wide, tags = prepare(
        qown, qother, page_dest.reshape(1, pages), page_row.reshape(1, pages), mine,
        owners * SLOT, n,
    )
    top, mass, acc = resident(
        queries,
        kv_pool.reshape(-1, kv_pool.shape[2]),
        block_table.T,
        ctx_len.reshape(1, rows),
        new_kv,
    )
    probs, ext = score(*keys, qpage, wide, tags)
    sent = value(*values, probs, ext, psel)
    got = lax.all_to_all(sent.reshape(owners, 2 * SLOT, -1), OWN, 0, 0, tiled=True)
    return merge(got.reshape(owners * SLOT * 2, -1), top, mass, acc, rows)


def solution(mesh):
    split = Mesh(
        mesh.devices.reshape(mesh.shape["section"], mesh.shape["rep"], 2, 4),
        ("section", "rep", "tp_0", "tp_1"),
    )
    tp = ("tp_0", "tp_1")
    placed = (
        P(OWN, tp),
        P(tp),
        P(tp, None),
        P(OWN, None),
        P(OWN),
        P(OWN, tp),
        P(OWN, None, tp),
        P(OWN, None),
        P(OWN),
        P(OWN, tp),
    )

    return jax.shard_map(body, mesh=split, in_specs=placed, out_specs=P(OWN, tp), check_vma=False)
```

profile of v0, /device:TPU:1, one launch (start us, length us, event | category | flops | bytes accessed | tf_op | source)
XLA Modules:
  0.0 97.1 jit_solution(5026997908711944336)
XLA Ops:
  0.0 0.7 copy-done.5
  0.7 8.8 %shard_map.100 = (bf16[1040,128]{1,0:T(8,128)(2,1)S(1)}, bf16[1040,128]{1,0:T(8,128)(2,1)}, bf16[1040,128]{1,0:T(8,128)(2,1)S(1)}, bf16[1040,128]{1,0:T(8,128)(2...) custom-call(bf16[1024,1024]{1,0:T(8,128)(2,1)} %tok.1, ...), custom_call_target="tpu_custom_call" | custom-call | tf_op jit(solution)/shard_map/pallas_call | solution.py:117
  9.6 2.1 %collective-permute-start.8 = (bf16[1040,128]{1,0:T(8,128)(2,1)S(1)}, bf16[1040,128]{1,0:T(8,128)(2,1)S(1)}, u32[]{:S(2)}, u32[]{:S(2)}) collective-permute-start(bf16[1040,128]{1,0:T(8,128)(2,1)S(1)} %get-tuple-element.52), channel_id=1, source_target_pairs={{0,1},{1,0},{2,3},{3,2},{4,5},{5,4},{6,7},{7,6},{8,9},{9,8},{10,11... | collective-permute-start | bytes 798728 | tf_op jit(solution)/shard_map/ppermute | solution.py:418
  11.7 1.8 %collective-permute-start.9 = (bf16[1040,128]{1,0:T(8,128)(2,1)S(1)}, bf16[1040,128]{1,0:T(8,128)(2,1)S(1)}, u32[]{:S(2)}, u32[]{:S(2)}) collective-permute-start(bf16[1040,128]{1,0:T(8,128)(2,1)S(1)} %get-tuple-element.54), channel_id=1, source_target_pairs={{0,3},{3,0},{1,2},{2,1},{4,7},{7,4},{5,6},{6,5},{8,11},{11,8},{9,1... | collective-permute-start | bytes 798728 | tf_op jit(solution)/shard_map/ppermute | solution.py:418
  13.8 1.2 %collective-permute-start.7 = (bf16[1040,128]{1,0:T(8,128)(2,1)}, bf16[1040,128]{1,0:T(8,128)(2,1)S(1)}, u32[]{:S(2)}, u32[]{:S(2)}) collective-permute-start(bf16[1040,128]{1,0:T(8,128)(2,1)} %get-tuple-element.50), channel_id=1, source_target_pairs={{0,1},{1,0},{2,3},{3,2},{4,5},{5,4},{6,7},{7,6},{8,9},{9,8},{10,11... | collective-permute-start | bytes 798728 | tf_op jit(solution)/shard_map/ppermute | solution.py:419
  15.0 0.9 collective-permute-start.11
  15.8 0.7 collective-permute-done.8.a0
  16.5 3.0 %collective-permute-done.9.b0 = bf16[1040,128]{1,0:T(8,128)(2,1)S(1)} collective-permute-done((bf16[1040,128]{1,0:T(8,128)(2,1)S(1)}, bf16[1040,128]{1,0:T(8,128)(2,1)S(1)}, u32[]{:S(2)}, u32[]{:S(2)}) %collective-permute-start.9) | collective-permute-done | bytes 266272 | tf_op jit(solution)/shard_map/ppermute | solution.py:418
  19.6 0.8 shard_map.103
  20.4 2.1 %collective-permute-start.10 = (bf16[1040,128]{1,0:T(8,128)(2,1)}, bf16[1040,128]{1,0:T(8,128)(2,1)S(1)}, u32[]{:S(2)}, u32[]{:S(2)}) collective-permute-start(bf16[1040,128]{1,0:T(8,128)(2,1)} %get-tuple-element.56), channel_id=1, source_target_pairs={{0,3},{3,0},{1,2},{2,1},{4,7},{7,4},{5,6},{6,5},{8,11},{11,8},{9,1... | collective-permute-start | bytes 798728 | tf_op jit(solution)/shard_map/ppermute | solution.py:421
  22.5 0.7 collective-permute-start.2
  23.3 0.7 broadcast_in_dim.2
  24.0 8.7 %all-to-all-start = ((bf16[16,8,1024]{2,1,0:T(8,128)(2,1)}), bf16[16,8,1024]{2,1,0:T(8,128)(2,1)S(1)}, u32[]{:S(2)}, u32[]{:S(2)}) async-start(bf16[16,8,1024]{2,1,0:T(8,128)(2,1)} %broadcast_in_dim.2), calls=%async_computation | async-start | bytes 524288 | tf_op jit(solution)/shard_map/all_to_all | solution.py:428
  32.8 3.7 %collective-permute-done.2.b0 = bf16[1024,128]{1,0:T(8,128)(2,1)S(1)} collective-permute-done((bf16[1024,128]{1,0:T(8,128)(2,1)}, bf16[1024,128]{1,0:T(8,128)(2,1)S(1)}, u32[]{:S(2)}, u32[]{:S(2)}) %collective-permute-start.2) | collective-permute-done | bytes 262176 | tf_op jit(solution)/shard_map/ppermute | solution.py:422
  36.5 0.7 copy-done.1
  37.2 0.9 copy-done.2
  38.1 0.9 shard_map.101
  39.1 2.1 %collective-permute-start.4 = (bf16[1024,128]{1,0:T(8,128)(2,1)}, bf16[1024,128]{1,0:T(8,128)(2,1)S(1)}, u32[]{:S(2)}, u32[]{:S(2)}) collective-permute-start(bf16[1024,128]{1,0:T(8,128)(2,1)} %copy-done.11), channel_id=1, source_target_pairs={{0,3},{3,0},{1,2},{2,1},{4,7},{7,4},{5,6},{6,5},{8,11},{11,8},{9,1... | collective-permute-start | bytes 786440 | tf_op jit(solution)/shard_map/ppermute | solution.py:423
  41.2 0.5 collective-permute-start.3
  41.7 0.6 collective-permute-start.5
  42.3 1.0 %shard_map.104 = (bf16[1040,128]{1,0:T(8,128)(2,1)}, bf16[1040,128]{1,0:T(8,128)(2,1)S(1)}) custom-call(bf16[1040,128]{1,0:T(8,128)(2,1)S(1)} %collective-permute-done.7.a0, bf16[1040,128]{1,0:T(8,128)(2,1)S(1)} %get-tuple-element.51.a1, bf16[1040,128]{1,0:T(8,128)(2,1)S(1)} %collective-permute-done.10.a2, bf16[1040,128]{1,0:T(8,128)(2,1)S(1)} %collective-permute-done.11.b0, ...), custom_call_target="tpu_custom_call" | custom-call | tf_op jit(solution)/shard_map/pallas_call | solution.py:158
  43.4 6.9 %collective-permute-start.13 = (bf16[1040,128]{1,0:T(8,128)(2,1)}, bf16[1040,128]{1,0:T(8,128)(2,1)S(1)}, u32[]{:S(2)}, u32[]{:S(2)}) collective-permute-start(bf16[1040,128]{1,0:T(8,128)(2,1)} %get-tuple-element.60), channel_id=1, source_target_pairs={{0,4},{4,0},{1,5},{5,1},{2,6},{6,2},{3,7},{7,3},{8,12},{12,8},{9,1... | collective-permute-start | bytes 798728 | tf_op jit(solution)/shard_map/ppermute | solution.py:433
  50.3 3.3 %collective-permute-start.14 = (bf16[128,1024]{1,0:T(8,128)(2,1)S(1)}, bf16[128,1024]{1,0:T(8,128)(2,1)S(1)}, u32[]{:S(2)}, u32[]{:S(2)}) collective-permute-start(bf16[128,1024]{1,0:T(8,128)(2,1)S(1)} %bitcast.10), channel_id=1, source_target_pairs={{0,128},{128,0},{1,129},{129,1},{2,130},{130,2},{3,131},{131,3},{4... | collective-permute-start | bytes 786440 | tf_op jit(solution)/shard_map/ppermute | solution.py:429
  53.6 2.0 %shard_map.102 = (bf16[1024,128]{1,0:T(8,128)(2,1)}, bf16[1024,128]{1,0:T(8,128)(2,1)S(1)}) custom-call(bf16[1024,128]{1,0:T(8,128)(2,1)S(1)} %collective-permute-done.a0, bf16[1024,128]{1,0:T(8,128)(2,1)S(1)} %get-tuple-element.39.a1, bf16[1024,128]{1,0:T(8,128)(2,1)S(1)} %collective-permute-done.3.a2, bf16[1024,128]{1,0:T(8,128)(2,1)S(1)} %collective-permute-done.4.b0, ...), custom_call_target="tpu_custom_call" | custom-call | tf_op jit(solution)/shard_map/pallas_call | solution.py:158
  55.6 5.7 %collective-permute-start.6 = (bf16[1024,128]{1,0:T(8,128)(2,1)}, bf16[1024,128]{1,0:T(8,128)(2,1)S(1)}, u32[]{:S(2)}, u32[]{:S(2)}) collective-permute-start(bf16[1024,128]{1,0:T(8,128)(2,1)} %get-tuple-element.48), channel_id=1, source_target_pairs={{0,4},{4,0},{1,5},{5,1},{2,6},{6,2},{3,7},{7,3},{8,12},{12,8},{9,1... | collective-permute-start | bytes 786440 | tf_op jit(solution)/shard_map/ppermute | solution.py:435
  61.3 0.5 prepare.1
  61.8 1.2 %score.1 = (f32[8,1024]{1,0:T(8,128)S(1)}, bf16[256,128]{1,0:T(8,128)(2,1)S(1)}) custom-call(bf16[1040,128]{1,0:T(8,128)(2,1)S(1)} %collective-permute-done.13.keys0, bf16[1040,128]{1,0:T(8,128)(2,1)S(1)} %get-tuple-element.61.keys1, bf16[512,128]{1,0:T(8,128)(2,1)S(1)} %get-tuple-element.62.qpage, bf16[256,1024]{1,0:T(8,128)(2,1)S(1)} %get-tuple-element.63.wide, ...), custom_call_target="tpu_custom_call" | custom-call | tf_op jit(solution)/shard_map/score/pallas_call | solution.py:272
  63.0 13.0 %collective-permute-done.6.values0 = bf16[1024,128]{1,0:T(8,128)(2,1)S(1)} collective-permute-done((bf16[1024,128]{1,0:T(8,128)(2,1)}, bf16[1024,128]{1,0:T(8,128)(2,1)S(1)}, u32[]{:S(2)}, u32[]{:S(2)}) %collective-permute-start.6) | collective-permute-done | bytes 262176 | tf_op jit(solution)/shard_map/ppermute | solution.py:435
  76.0 1.2 %value.1 = bf16[256,640]{1,0:T(8,128)(2,1)} custom-call(bf16[1024,128]{1,0:T(8,128)(2,1)S(1)} %collective-permute-done.6.values0, bf16[1024,128]{1,0:T(8,128)(2,1)S(1)} %get-tuple-element.49.values1, f32[8,1024]{1,0:T(8,128)S(1)} %get-tuple-element.65.probs, bf16[256,128]{1,0:T(8,128)(2,1)S(1)} %get-tuple-element.66.ext, ...), custom_call_target="tpu_custom_call" | custom-call | tf_op jit(solution)/shard_map/value/pallas_call | solution.py:310
  77.3 6.6 %all-to-all-start.1 = ((bf16[32,8,640]{2,1,0:T(8,128)(2,1)}), bf16[32,8,640]{2,1,0:T(8,128)(2,1)S(1)}, u32[]{:S(2)}, u32[]{:S(2)}) async-start(bf16[32,8,640]{2,1,0:T(8,128)(2,1)} %bitcast.4), calls=%async_computation.1 | async-start | bytes 655360 | tf_op jit(solution)/shard_map/all_to_all | solution.py:452
  84.3 11.7 %all-to-all-done.1 = bf16[32,8,640]{2,1,0:T(8,128)(2,1)S(1)} async-done(((bf16[32,8,640]{2,1,0:T(8,128)(2,1)}), bf16[32,8,640]{2,1,0:T(8,128)(2,1)S(1)}, u32[]{:S(2)}, u32[]{:S(2)}) %all-to-all-start.1) | async-done | bytes 327712 | tf_op jit(solution)/shard_map/all_to_all | solution.py:452
  96.1 1.1 %merge.1 = bf16[8,1024]{1,0:T(8,128)(2,1)} custom-call(bf16[256,640]{1,0:T(8,128)(2,1)S(1)} %bitcast.9, f32[64,1]{1,0:T(8,128)S(1)} %get-tuple-element.68.top_in, f32[64,1]{1,0:T(8,128)S(1)} %get-tuple-element.69.mass_in, f32[64,128]{1,0:T(8,128)S(1)} %get-tuple-element.70.acc_in), custom_call_target="tpu_custom_call" | custom-call | tf_op jit(solution)/shard_map/merge/pallas_call | solution.py:384
  (39 shorter events, 0.9 us)
Async XLA Ops:
  0.0 23.3 %copy-start.3 = (bf16[8,1024]{1,0:T(8,128)(2,1)S(1)}, bf16[8,1024]{1,0:T(8,128)(2,1)}, u32[]{:S(2)}) copy-start(bf16[8,1024]{1,0:T(8,128)(2,1)} %queries.1) | copy-start | bytes 49156
  0.0 0.7 copy-start.5
  9.5 13.7 %copy-start.11 = (bf16[1024,128]{1,0:T(8,128)(2,1)}, bf16[1024,128]{1,0:T(8,128)(2,1)S(1)}, u32[]{:S(2)}) copy-start(bf16[1024,128]{1,0:T(8,128)(2,1)S(1)} %get-tuple-element.45) | copy-start | bytes 786436
  9.5 13.7 %copy-start.12 = (bf16[1024,128]{1,0:T(8,128)(2,1)}, bf16[1024,128]{1,0:T(8,128)(2,1)S(1)}, u32[]{:S(2)}) copy-start(bf16[1024,128]{1,0:T(8,128)(2,1)S(1)} %get-tuple-element.38) | copy-start | bytes 786436
  9.5 51.8 %copy-start.7 = (s32[64,1]{0,1:T(1,128)S(1)}, s32[64,1]{0,1:T(1,128)}, u32[]{:S(2)}) copy-start(s32[64,1]{0,1:T(1,128)} %param.13) | copy-start | bytes 772
  9.6 51.8 %copy-start.8 = (s32[64]{0:T(128)S(1)}, s32[64]{0:T(128)}, u32[]{:S(2)}) copy-start(s32[64]{0:T(128)} %param.14) | copy-start | bytes 772
  9.6 7.0 %collective-permute-start.8 = (bf16[1040,128]{1,0:T(8,128)(2,1)S(1)}, bf16[1040,128]{1,0:T(8,128)(2,1)S(1)}, u32[]{:S(2)}, u32[]{:S(2)}) collective-permute-start(bf16[1040,128]{1,0:T(8,128)(2,1)S(1)} %get-tuple-element.52), channel_id=1, source_target_pairs={{0,1},{1,0},{2,3},{3,2},{4,5},{5,4},{6,7},{7,6},{8,9},{9,8},{10,11... | collective-permute-start | bytes 798728 | tf_op jit(solution)/shard_map/ppermute | solution.py:418
  11.7 7.9 %collective-permute-start.9 = (bf16[1040,128]{1,0:T(8,128)(2,1)S(1)}, bf16[1040,128]{1,0:T(8,128)(2,1)S(1)}, u32[]{:S(2)}, u32[]{:S(2)}) collective-permute-start(bf16[1040,128]{1,0:T(8,128)(2,1)S(1)} %get-tuple-element.54), channel_id=1, source_target_pairs={{0,3},{3,0},{1,2},{2,1},{4,7},{7,4},{5,6},{6,5},{8,11},{11,8},{9,1... | collective-permute-start | bytes 798728 | tf_op jit(solution)/shard_map/ppermute | solution.py:418
  13.5 19.2 %collective-permute-start.1 = (bf16[1024,128]{1,0:T(8,128)(2,1)}, bf16[1024,128]{1,0:T(8,128)(2,1)S(1)}, u32[]{:S(2)}, u32[]{:S(2)}) collective-permute-start(bf16[1024,128]{1,0:T(8,128)(2,1)} %get-tuple-element.40), channel_id=1, source_target_pairs={{0,1},{1,0},{2,3},{3,2},{4,5},{5,4},{6,7},{7,6},{8,9},{9,8},{10,11... | collective-permute-start | bytes 786440 | tf_op jit(solution)/shard_map/ppermute | solution.py:422
  13.8 25.2 %collective-permute-start.7 = (bf16[1040,128]{1,0:T(8,128)(2,1)}, bf16[1040,128]{1,0:T(8,128)(2,1)S(1)}, u32[]{:S(2)}, u32[]{:S(2)}) collective-permute-start(bf16[1040,128]{1,0:T(8,128)(2,1)} %get-tuple-element.50), channel_id=1, source_target_pairs={{0,1},{1,0},{2,3},{3,2},{4,5},{5,4},{6,7},{7,6},{8,9},{9,8},{10,11... | collective-permute-start | bytes 798728 | tf_op jit(solution)/shard_map/ppermute | solution.py:419
  15.0 26.2 %collective-permute-start.11 = (bf16[1040,128]{1,0:T(8,128)(2,1)}, bf16[1040,128]{1,0:T(8,128)(2,1)S(1)}, u32[]{:S(2)}, u32[]{:S(2)}) collective-permute-start(bf16[1040,128]{1,0:T(8,128)(2,1)} %get-tuple-element.57), channel_id=1, source_target_pairs={{0,3},{3,0},{1,2},{2,1},{4,7},{7,4},{5,6},{6,5},{8,11},{11,8},{9,1... | collective-permute-start | bytes 798728 | tf_op jit(solution)/shard_map/ppermute | solution.py:419
  20.4 2.1 %copy-start.10 = (bf16[1040,128]{1,0:T(8,128)(2,1)}, bf16[1040,128]{1,0:T(8,128)(2,1)S(1)}, u32[]{:S(2)}) copy-start(bf16[1040,128]{1,0:T(8,128)(2,1)S(1)} %get-tuple-element.59) | copy-start | bytes 798724
  20.4 21.3 %collective-permute-start.10 = (bf16[1040,128]{1,0:T(8,128)(2,1)}, bf16[1040,128]{1,0:T(8,128)(2,1)S(1)}, u32[]{:S(2)}, u32[]{:S(2)}) collective-permute-start(bf16[1040,128]{1,0:T(8,128)(2,1)} %get-tuple-element.56), channel_id=1, source_target_pairs={{0,3},{3,0},{1,2},{2,1},{4,7},{7,4},{5,6},{6,5},{8,11},{11,8},{9,1... | collective-permute-start | bytes 798728 | tf_op jit(solution)/shard_map/ppermute | solution.py:421
  22.5 14.0 %collective-permute-start.2 = (bf16[1024,128]{1,0:T(8,128)(2,1)}, bf16[1024,128]{1,0:T(8,128)(2,1)S(1)}, u32[]{:S(2)}, u32[]{:S(2)}) collective-permute-start(bf16[1024,128]{1,0:T(8,128)(2,1)} %get-tuple-element.42), channel_id=1, source_target_pairs={{0,3},{3,0},{1,2},{2,1},{4,7},{7,4},{5,6},{6,5},{8,11},{11,8},{9,1... | collective-permute-start | bytes 786440 | tf_op jit(solution)/shard_map/ppermute | solution.py:422
  24.0 59.9 %copy-start = (bf16[32,16,256]{2,1,0:T(8,128)(2,1)S(1)}, bf16[32,16,256]{2,1,0:T(8,128)(2,1)}, u32[]{:S(2)}) copy-start(bf16[32,16,256]{2,1,0:T(8,128)(2,1)} %param.16) | copy-start | bytes 786436
  24.0 59.9 %copy-start.4 = (bf16[8,256]{1,0:T(8,128)(2,1)S(1)}, bf16[8,256]{1,0:T(8,128)(2,1)}, u32[]{:S(2)}) copy-start(bf16[8,256]{1,0:T(8,128)(2,1)} %fresh.1) | copy-start | bytes 12292
  24.0 59.9 %copy-start.6 = (s32[8,4]{0,1:T(4,128)S(1)}, s32[8,4]{0,1:T(4,128)}, u32[]{:S(2)}) copy-start(s32[8,4]{0,1:T(4,128)} %param.17) | copy-start | bytes 388
  24.0 59.9 %copy-start.9 = (s32[8]{0:T(128)S(1)}, s32[8]{0:T(128)}, u32[]{:S(2)}) copy-start(s32[8]{0:T(128)} %param.18) | copy-start | bytes 100
  24.0 26.3 %all-to-all-start = ((bf16[16,8,1024]{2,1,0:T(8,128)(2,1)}), bf16[16,8,1024]{2,1,0:T(8,128)(2,1)S(1)}, u32[]{:S(2)}, u32[]{:S(2)}) async-start(bf16[16,8,1024]{2,1,0:T(8,128)(2,1)} %broadcast_in_dim.2), calls=%async_computation | async-start | bytes 524288 | tf_op jit(solution)/shard_map/all_to_all | solution.py:428
  32.7 9.7 %collective-permute-start.12 = (bf16[1040,128]{1,0:T(8,128)(2,1)}, bf16[1040,128]{1,0:T(8,128)(2,1)S(1)}, u32[]{:S(2)}, u32[]{:S(2)}) collective-permute-start(bf16[1040,128]{1,0:T(8,128)(2,1)} %copy-done.10), channel_id=1, source_target_pairs={{0,1},{1,0},{2,3},{3,2},{4,5},{5,4},{6,7},{7,6},{8,9},{9,8},{10,11... | collective-permute-start | bytes 798728 | tf_op jit(solution)/shard_map/ppermute | solution.py:421
  36.5 0.7 copy-start.1
  37.2 13.1 %collective-permute-start = (bf16[1024,128]{1,0:T(8,128)(2,1)}, bf16[1024,128]{1,0:T(8,128)(2,1)S(1)}, u32[]{:S(2)}, u32[]{:S(2)}) collective-permute-start(bf16[1024,128]{1,0:T(8,128)(2,1)} %copy-done.12), channel_id=1, source_target_pairs={{0,1},{1,0},{2,3},{3,2},{4,5},{5,4},{6,7},{7,6},{8,9},{9,8},{10,11... | collective-permute-start | bytes 786440 | tf_op jit(solution)/shard_map/ppermute | solution.py:423
  37.2 1.0 copy-start.2
  39.1 14.5 %collective-permute-start.4 = (bf16[1024,128]{1,0:T(8,128)(2,1)}, bf16[1024,128]{1,0:T(8,128)(2,1)S(1)}, u32[]{:S(2)}, u32[]{:S(2)}) collective-permute-start(bf16[1024,128]{1,0:T(8,128)(2,1)} %copy-done.11), channel_id=1, source_target_pairs={{0,3},{3,0},{1,2},{2,1},{4,7},{7,4},{5,6},{6,5},{8,11},{11,8},{9,1... | collective-permute-start | bytes 786440 | tf_op jit(solution)/shard_map/ppermute | solution.py:423
  41.2 12.4 %collective-permute-start.3 = (bf16[1024,128]{1,0:T(8,128)(2,1)}, bf16[1024,128]{1,0:T(8,128)(2,1)S(1)}, u32[]{:S(2)}, u32[]{:S(2)}) collective-permute-start(bf16[1024,128]{1,0:T(8,128)(2,1)} %get-tuple-element.44), channel_id=1, source_target_pairs={{0,3},{3,0},{1,2},{2,1},{4,7},{7,4},{5,6},{6,5},{8,11},{11,8},{9,1... | collective-permute-start | bytes 786440 | tf_op jit(solution)/shard_map/ppermute | solution.py:431
  41.7 11.9 %collective-permute-start.5 = (bf16[1024,128]{1,0:T(8,128)(2,1)}, bf16[1024,128]{1,0:T(8,128)(2,1)}, u32[]{:S(2)}, u32[]{:S(2)}) collective-permute-start(bf16[1024,128]{1,0:T(8,128)(2,1)} %get-tuple-element.47), channel_id=1, source_target_pairs={{0,1},{1,0},{2,3},{3,2},{4,5},{5,4},{6,7},{7,6},{8,9},{9,8},{10,11... | collective-permute-start | bytes 786440 | tf_op jit(solution)/shard_map/ppermute | solution.py:431
  43.4 18.4 %collective-permute-start.13 = (bf16[1040,128]{1,0:T(8,128)(2,1)}, bf16[1040,128]{1,0:T(8,128)(2,1)S(1)}, u32[]{:S(2)}, u32[]{:S(2)}) collective-permute-start(bf16[1040,128]{1,0:T(8,128)(2,1)} %get-tuple-element.60), channel_id=1, source_target_pairs={{0,4},{4,0},{1,5},{5,1},{2,6},{6,2},{3,7},{7,3},{8,12},{12,8},{9,1... | collective-permute-start | bytes 798728 | tf_op jit(solution)/shard_map/ppermute | solution.py:433
  50.3 11.0 %collective-permute-start.14 = (bf16[128,1024]{1,0:T(8,128)(2,1)S(1)}, bf16[128,1024]{1,0:T(8,128)(2,1)S(1)}, u32[]{:S(2)}, u32[]{:S(2)}) collective-permute-start(bf16[128,1024]{1,0:T(8,128)(2,1)S(1)} %bitcast.10), channel_id=1, source_target_pairs={{0,128},{128,0},{1,129},{129,1},{2,130},{130,2},{3,131},{131,3},{4... | collective-permute-start | bytes 786440 | tf_op jit(solution)/shard_map/ppermute | solution.py:429
  55.6 20.4 %collective-permute-start.6 = (bf16[1024,128]{1,0:T(8,128)(2,1)}, bf16[1024,128]{1,0:T(8,128)(2,1)S(1)}, u32[]{:S(2)}, u32[]{:S(2)}) collective-permute-start(bf16[1024,128]{1,0:T(8,128)(2,1)} %get-tuple-element.48), channel_id=1, source_target_pairs={{0,4},{4,0},{1,5},{5,1},{2,6},{6,2},{3,7},{7,3},{8,12},{12,8},{9,1... | collective-permute-start | bytes 786440 | tf_op jit(solution)/shard_map/ppermute | solution.py:435
  77.3 18.8 %all-to-all-start.1 = ((bf16[32,8,640]{2,1,0:T(8,128)(2,1)}), bf16[32,8,640]{2,1,0:T(8,128)(2,1)S(1)}, u32[]{:S(2)}, u32[]{:S(2)}) async-start(bf16[32,8,640]{2,1,0:T(8,128)(2,1)} %bitcast.4), calls=%async_computation.1 | async-start | bytes 655360 | tf_op jit(solution)/shard_map/all_to_all | solution.py:452
where the time goes:
time: 97.5 us; the launch traced here: 97.1 us
  starting transfers between devices  43.6 us (45%)
  waiting for transfers between devices  32.3 us (33%)
  Pallas kernels  18 us (18%)
  local copies, waits for them, and re-layouts  3.1 us (3%)
    ppermute x1, waiting for transfers between devices, body(): values = (lax.ppermute(give, 'tp_0', SWAP), keep)  13 us
    all_to_all x1, waiting for transfers between devices, body(): lax.all_to_all(sent.reshape(owners, 2 * SLOT, -1), OWN, 0, 0, tiled=True)  11.7 us
    pallas_call x1, Pallas kernels, projection(): pl.pallas_call(kernel, in_specs=[hbm, hbm, hbm] + [vmem for _ in extra],...  8.82 us
    all_to_all x1, starting transfers between devices, body(): lax.all_to_all(spread, 'rep', 0, 0, tiled=True).reshape(peers * rows, -1)  8.65 us
    ppermute x1, starting transfers between devices, body(): keys = (lax.ppermute(give, 'tp_0', SWAP), keep)  6.91 us
    all_to_all x1, starting transfers between devices, body(): lax.all_to_all(sent.reshape(owners, 2 * SLOT, -1), OWN, 0, 0, tiled=True)  6.64 us
    ppermute x1, starting transfers between devices, body(): values = (lax.ppermute(give, 'tp_0', SWAP), keep)  5.67 us
    ppermute x1, waiting for transfers between devices, body(): lax.ppermute(vf_b, 'tp_1', FAR)  3.74 us
  transfers between devices with their start and end apart: 17, of which 5 were waited for; matrix products, arithmetic and copies ran while one was open for 1% of the time, Pallas kernels for 7%

commit v1 on v0

--- a/solution.py
+++ b/solution.py
@@ -107,7 +107,7 @@
         c.wait()
 
 
-VM = 48 << 20
+VM = 50 << 20
 
 
 def projection(kernel, count, chunks, tokens, gain, weight, extra, shapes, scratch, outs, sems):
@@ -122,7 +122,10 @@
         + scratch
         + [pltpu.SemaphoreType.DMA((chunks,)), pltpu.SemaphoreType.DMA((count,))]
         + sems,
-        out_shape=[jax.ShapeDtypeStruct(s, BF) for s in shapes],
+        out_shape=[
+            pltpu.HBM(s, BF) if o.memory_space == pltpu.HBM else jax.ShapeDtypeStruct(s, BF)
+            for s, o in zip(shapes, outs)
+        ],
         compiler_params=pltpu.CompilerParams(vmem_limit_bytes=VM),
     )(tokens, gain, weight, *extra)
 
@@ -410,7 +413,7 @@
         kf_a, ko_a, kf_b, ko_b, vf_a, vo_a, vf_b, vo_b,
         kkf_a, kko_a, kkf_b, kko_b, vkf_a, vko_a, vkf_b, vko_b,
     ) = projection(
-        project_kernel, 16, 4, tokens, gain, kv_weight, [],
+        project_kernel, 16, 2, tokens, gain, kv_weight, [],
         [ext] * 4 + [one] * 4 + [ext] * 4 + [one] * 4,
         [pltpu.VMEM((8, *ext), BF), pltpu.VMEM((8, n), F32), pltpu.VMEM((d,), BF)], [hbm] * 8 + [vmem] * 8,
         [pltpu.SemaphoreType.DMA((8,)), pltpu.SemaphoreType.DMA],

time: 97.5 us -> 97.6 us (level)
    unnamed x26 -> x22, local copies, waits for them, and re-layouts: 2.38 us -> 2.38 us
where the time goes in v1:
time: 97.6 us; the launch traced here: 97.2 us
  starting transfers between devices  43.6 us (45%)
  waiting for transfers between devices  32.5 us (33%)
  Pallas kernels  17.9 us (18%)
  local copies, waits for them, and re-layouts  3.1 us (3%)
    ppermute x1, waiting for transfers between devices, body(): values = (lax.ppermute(give, 'tp_0', SWAP), keep)  13 us
    all_to_all x1, waiting for transfers between devices, body(): lax.all_to_all(sent.reshape(owners, 2 * SLOT, -1), OWN, 0, 0, tiled=True)  11.7 us
    pallas_call x1, Pallas kernels, projection(): pl.pallas_call(kernel, in_specs=[hbm, hbm, hbm] + [vmem for _ in extra],...  8.74 us
    all_to_all x1, starting transfers between devices, body(): lax.all_to_all(spread, 'rep', 0, 0, tiled=True).reshape(peers * rows, -1)  8.67 us
    ppermute x1, starting transfers between devices, body(): keys = (lax.ppermute(give, 'tp_0', SWAP), keep)  7.08 us
    all_to_all x1, starting transfers between devices, body(): lax.all_to_all(sent.reshape(owners, 2 * SLOT, -1), OWN, 0, 0, tiled=True)  6.63 us
    ppermute x1, starting transfers between devices, body(): values = (lax.ppermute(give, 'tp_0', SWAP), keep)  5.66 us
    ppermute x1, waiting for transfers between devices, body(): lax.ppermute(vf_b, 'tp_1', FAR)  3.76 us
  transfers between devices with their start and end apart: 17, of which 5 were waited for; matrix products, arithmetic and copies ran while one was open for 1% of the time, Pallas kernels for 7%

profile of v1, /device:TPU:1, one launch (start us, length us, event | category | flops | bytes accessed | tf_op | source)
XLA Modules:
  0.0 97.2 jit_solution(15921064280638932819)
XLA Ops:
  0.0 0.7 copy-done.5
  0.7 8.7 %shard_map.100 = (bf16[1040,128]{1,0:T(8,128)(2,1)}, bf16[1040,128]{1,0:T(8,128)(2,1)}, bf16[1040,128]{1,0:T(8,128)(2,1)}, bf16[1040,128]{1,0:T(8,128)(2,1)}, bf...) custom-call(bf16[1024,1024]{1,0:T(8,128)(2,1)} %tok.1, ...), custom_call_target="tpu_custom_call" | custom-call | tf_op jit(solution)/shard_map/pallas_call | solution.py:117
  9.5 2.1 %collective-permute-start.8 = (bf16[1040,128]{1,0:T(8,128)(2,1)}, bf16[1040,128]{1,0:T(8,128)(2,1)S(1)}, u32[]{:S(2)}, u32[]{:S(2)}) collective-permute-start(bf16[1040,128]{1,0:T(8,128)(2,1)} %get-tuple-element.52), channel_id=1, source_target_pairs={{0,1},{1,0},{2,3},{3,2},{4,5},{5,4},{6,7},{7,6},{8,9},{9,8},{10,11... | collective-permute-start | bytes 798728 | tf_op jit(solution)/shard_map/ppermute | solution.py:421
  11.6 1.8 %collective-permute-start.9 = (bf16[1040,128]{1,0:T(8,128)(2,1)}, bf16[1040,128]{1,0:T(8,128)(2,1)S(1)}, u32[]{:S(2)}, u32[]{:S(2)}) collective-permute-start(bf16[1040,128]{1,0:T(8,128)(2,1)} %get-tuple-element.54), channel_id=1, source_target_pairs={{0,3},{3,0},{1,2},{2,1},{4,7},{7,4},{5,6},{6,5},{8,11},{11,8},{9,1... | collective-permute-start | bytes 798728 | tf_op jit(solution)/shard_map/ppermute | solution.py:421
  13.7 1.1 %collective-permute-start.7 = (bf16[1040,128]{1,0:T(8,128)(2,1)}, bf16[1040,128]{1,0:T(8,128)(2,1)S(1)}, u32[]{:S(2)}, u32[]{:S(2)}) collective-permute-start(bf16[1040,128]{1,0:T(8,128)(2,1)} %get-tuple-element.50), channel_id=1, source_target_pairs={{0,1},{1,0},{2,3},{3,2},{4,5},{5,4},{6,7},{7,6},{8,9},{9,8},{10,11... | collective-permute-start | bytes 798728 | tf_op jit(solution)/shard_map/ppermute | solution.py:422
  14.9 0.9 collective-permute-start.11
  15.7 1.0 %collective-permute-done.8.a0 = bf16[1040,128]{1,0:T(8,128)(2,1)S(1)} collective-permute-done((bf16[1040,128]{1,0:T(8,128)(2,1)}, bf16[1040,128]{1,0:T(8,128)(2,1)S(1)}, u32[]{:S(2)}, u32[]{:S(2)}) %collective-permute-start.8) | collective-permute-done | bytes 266272 | tf_op jit(solution)/shard_map/ppermute | solution.py:421
  16.8 2.9 %collective-permute-done.9.b0 = bf16[1040,128]{1,0:T(8,128)(2,1)S(1)} collective-permute-done((bf16[1040,128]{1,0:T(8,128)(2,1)}, bf16[1040,128]{1,0:T(8,128)(2,1)S(1)}, u32[]{:S(2)}, u32[]{:S(2)}) %collective-permute-start.9) | collective-permute-done | bytes 266272 | tf_op jit(solution)/shard_map/ppermute | solution.py:421
  19.7 0.8 shard_map.103
  20.5 2.1 %collective-permute-start.10 = (bf16[1040,128]{1,0:T(8,128)(2,1)}, bf16[1040,128]{1,0:T(8,128)(2,1)S(1)}, u32[]{:S(2)}, u32[]{:S(2)}) collective-permute-start(bf16[1040,128]{1,0:T(8,128)(2,1)} %get-tuple-element.56), channel_id=1, source_target_pairs={{0,3},{3,0},{1,2},{2,1},{4,7},{7,4},{5,6},{6,5},{8,11},{11,8},{9,1... | collective-permute-start | bytes 798728 | tf_op jit(solution)/shard_map/ppermute | solution.py:424
  22.6 0.7 collective-permute-start.2
  23.3 0.7 broadcast_in_dim.2
  24.1 8.7 %all-to-all-start = ((bf16[16,8,1024]{2,1,0:T(8,128)(2,1)}), bf16[16,8,1024]{2,1,0:T(8,128)(2,1)S(1)}, u32[]{:S(2)}, u32[]{:S(2)}) async-start(bf16[16,8,1024]{2,1,0:T(8,128)(2,1)} %broadcast_in_dim.2), calls=%async_computation | async-start | bytes 524288 | tf_op jit(solution)/shard_map/all_to_all | solution.py:431
  32.9 3.8 %collective-permute-done.2.b0 = bf16[1024,128]{1,0:T(8,128)(2,1)S(1)} collective-permute-done((bf16[1024,128]{1,0:T(8,128)(2,1)}, bf16[1024,128]{1,0:T(8,128)(2,1)S(1)}, u32[]{:S(2)}, u32[]{:S(2)}) %collective-permute-start.2) | collective-permute-done | bytes 262176 | tf_op jit(solution)/shard_map/ppermute | solution.py:425
  36.6 0.7 copy-done.1
  37.3 0.9 copy-done.2
  38.3 0.9 shard_map.101
  39.2 2.1 %collective-permute-start.4 = (bf16[1024,128]{1,0:T(8,128)(2,1)}, bf16[1024,128]{1,0:T(8,128)(2,1)S(1)}, u32[]{:S(2)}, u32[]{:S(2)}) collective-permute-start(bf16[1024,128]{1,0:T(8,128)(2,1)} %get-tuple-element.45), channel_id=1, source_target_pairs={{0,3},{3,0},{1,2},{2,1},{4,7},{7,4},{5,6},{6,5},{8,11},{11,8},{9,1... | collective-permute-start | bytes 786440 | tf_op jit(solution)/shard_map/ppermute | solution.py:426
  41.3 0.6 collective-permute-start.3
  41.9 0.4 collective-permute-start.5
  42.3 1.1 %shard_map.104 = (bf16[1040,128]{1,0:T(8,128)(2,1)}, bf16[1040,128]{1,0:T(8,128)(2,1)S(1)}) custom-call(bf16[1040,128]{1,0:T(8,128)(2,1)S(1)} %collective-permute-done.7.a0, bf16[1040,128]{1,0:T(8,128)(2,1)S(1)} %get-tuple-element.51.a1, bf16[1040,128]{1,0:T(8,128)(2,1)S(1)} %collective-permute-done.10.a2, bf16[1040,128]{1,0:T(8,128)(2,1)S(1)} %collective-permute-done.11.b0, ...), custom_call_target="tpu_custom_call" | custom-call | tf_op jit(solution)/shard_map/pallas_call | solution.py:161
  43.3 7.1 %collective-permute-start.13 = (bf16[1040,128]{1,0:T(8,128)(2,1)}, bf16[1040,128]{1,0:T(8,128)(2,1)S(1)}, u32[]{:S(2)}, u32[]{:S(2)}) collective-permute-start(bf16[1040,128]{1,0:T(8,128)(2,1)} %get-tuple-element.60), channel_id=1, source_target_pairs={{0,4},{4,0},{1,5},{5,1},{2,6},{6,2},{3,7},{7,3},{8,12},{12,8},{9,1... | collective-permute-start | bytes 798728 | tf_op jit(solution)/shard_map/ppermute | solution.py:436
  50.4 3.3 %collective-permute-start.14 = (bf16[128,1024]{1,0:T(8,128)(2,1)S(1)}, bf16[128,1024]{1,0:T(8,128)(2,1)S(1)}, u32[]{:S(2)}, u32[]{:S(2)}) collective-permute-start(bf16[128,1024]{1,0:T(8,128)(2,1)S(1)} %bitcast.10), channel_id=1, source_target_pairs={{0,128},{128,0},{1,129},{129,1},{2,130},{130,2},{3,131},{131,3},{4... | collective-permute-start | bytes 786440 | tf_op jit(solution)/shard_map/ppermute | solution.py:432
  53.7 2.0 %shard_map.102 = (bf16[1024,128]{1,0:T(8,128)(2,1)}, bf16[1024,128]{1,0:T(8,128)(2,1)S(1)}) custom-call(bf16[1024,128]{1,0:T(8,128)(2,1)S(1)} %collective-permute-done.a0, bf16[1024,128]{1,0:T(8,128)(2,1)S(1)} %get-tuple-element.39.a1, bf16[1024,128]{1,0:T(8,128)(2,1)S(1)} %collective-permute-done.3.a2, bf16[1024,128]{1,0:T(8,128)(2,1)S(1)} %collective-permute-done.4.b0, ...), custom_call_target="tpu_custom_call" | custom-call | tf_op jit(solution)/shard_map/pallas_call | solution.py:161
  55.7 5.7 %collective-permute-start.6 = (bf16[1024,128]{1,0:T(8,128)(2,1)}, bf16[1024,128]{1,0:T(8,128)(2,1)S(1)}, u32[]{:S(2)}, u32[]{:S(2)}) collective-permute-start(bf16[1024,128]{1,0:T(8,128)(2,1)} %get-tuple-element.48), channel_id=1, source_target_pairs={{0,4},{4,0},{1,5},{5,1},{2,6},{6,2},{3,7},{7,3},{8,12},{12,8},{9,1... | collective-permute-start | bytes 786440 | tf_op jit(solution)/shard_map/ppermute | solution.py:438
  61.4 0.5 prepare.1
  61.9 1.2 %score.1 = (f32[8,1024]{1,0:T(8,128)S(1)}, bf16[256,128]{1,0:T(8,128)(2,1)S(1)}) custom-call(bf16[1040,128]{1,0:T(8,128)(2,1)S(1)} %collective-permute-done.13.keys0, bf16[1040,128]{1,0:T(8,128)(2,1)S(1)} %get-tuple-element.61.keys1, bf16[512,128]{1,0:T(8,128)(2,1)S(1)} %get-tuple-element.62.qpage, bf16[256,1024]{1,0:T(8,128)(2,1)S(1)} %get-tuple-element.63.wide, ...), custom_call_target="tpu_custom_call" | custom-call | tf_op jit(solution)/shard_map/score/pallas_call | solution.py:275
  63.1 13.0 %collective-permute-done.6.values0 = bf16[1024,128]{1,0:T(8,128)(2,1)S(1)} collective-permute-done((bf16[1024,128]{1,0:T(8,128)(2,1)}, bf16[1024,128]{1,0:T(8,128)(2,1)S(1)}, u32[]{:S(2)}, u32[]{:S(2)}) %collective-permute-start.6) | collective-permute-done | bytes 262176 | tf_op jit(solution)/shard_map/ppermute | solution.py:438
  76.1 1.2 %value.1 = bf16[256,640]{1,0:T(8,128)(2,1)} custom-call(bf16[1024,128]{1,0:T(8,128)(2,1)S(1)} %collective-permute-done.6.values0, bf16[1024,128]{1,0:T(8,128)(2,1)S(1)} %get-tuple-element.49.values1, f32[8,1024]{1,0:T(8,128)S(1)} %get-tuple-element.65.probs, bf16[256,128]{1,0:T(8,128)(2,1)S(1)} %get-tuple-element.66.ext, ...), custom_call_target="tpu_custom_call" | custom-call | tf_op jit(solution)/shard_map/value/pallas_call | solution.py:313
  77.4 6.6 %all-to-all-start.1 = ((bf16[32,8,640]{2,1,0:T(8,128)(2,1)}), bf16[32,8,640]{2,1,0:T(8,128)(2,1)S(1)}, u32[]{:S(2)}, u32[]{:S(2)}) async-start(bf16[32,8,640]{2,1,0:T(8,128)(2,1)} %bitcast.4), calls=%async_computation.1 | async-start | bytes 655360 | tf_op jit(solution)/shard_map/all_to_all | solution.py:455
  84.4 11.7 %all-to-all-done.1 = bf16[32,8,640]{2,1,0:T(8,128)(2,1)S(1)} async-done(((bf16[32,8,640]{2,1,0:T(8,128)(2,1)}), bf16[32,8,640]{2,1,0:T(8,128)(2,1)S(1)}, u32[]{:S(2)}, u32[]{:S(2)}) %all-to-all-start.1) | async-done | bytes 327712 | tf_op jit(solution)/shard_map/all_to_all | solution.py:455
  96.1 1.1 %merge.1 = bf16[8,1024]{1,0:T(8,128)(2,1)} custom-call(bf16[256,640]{1,0:T(8,128)(2,1)S(1)} %bitcast.9, f32[64,1]{1,0:T(8,128)S(1)} %get-tuple-element.68.top_in, f32[64,1]{1,0:T(8,128)S(1)} %get-tuple-element.69.mass_in, f32[64,128]{1,0:T(8,128)S(1)} %get-tuple-element.70.acc_in), custom_call_target="tpu_custom_call" | custom-call | tf_op jit(solution)/shard_map/merge/pallas_call | solution.py:387
  (35 shorter events, 0.9 us)
Async XLA Ops:
  0.0 23.3 %copy-start.3 = (bf16[8,1024]{1,0:T(8,128)(2,1)S(1)}, bf16[8,1024]{1,0:T(8,128)(2,1)}, u32[]{:S(2)}) copy-start(bf16[8,1024]{1,0:T(8,128)(2,1)} %queries.1) | copy-start | bytes 49156
  0.0 0.7 copy-start.5
  9.4 52.0 %copy-start.7 = (s32[64,1]{0,1:T(1,128)S(1)}, s32[64,1]{0,1:T(1,128)}, u32[]{:S(2)}) copy-start(s32[64,1]{0,1:T(1,128)} %param.13) | copy-start | bytes 772
  9.5 52.0 %copy-start.8 = (s32[64]{0:T(128)S(1)}, s32[64]{0:T(128)}, u32[]{:S(2)}) copy-start(s32[64]{0:T(128)} %param.14) | copy-start | bytes 772
  9.5 7.3 %collective-permute-start.8 = (bf16[1040,128]{1,0:T(8,128)(2,1)}, bf16[1040,128]{1,0:T(8,128)(2,1)S(1)}, u32[]{:S(2)}, u32[]{:S(2)}) collective-permute-start(bf16[1040,128]{1,0:T(8,128)(2,1)} %get-tuple-element.52), channel_id=1, source_target_pairs={{0,1},{1,0},{2,3},{3,2},{4,5},{5,4},{6,7},{7,6},{8,9},{9,8},{10,11... | collective-permute-start | bytes 798728 | tf_op jit(solution)/shard_map/ppermute | solution.py:421
  11.6 8.1 %collective-permute-start.9 = (bf16[1040,128]{1,0:T(8,128)(2,1)}, bf16[1040,128]{1,0:T(8,128)(2,1)S(1)}, u32[]{:S(2)}, u32[]{:S(2)}) collective-permute-start(bf16[1040,128]{1,0:T(8,128)(2,1)} %get-tuple-element.54), channel_id=1, source_target_pairs={{0,3},{3,0},{1,2},{2,1},{4,7},{7,4},{5,6},{6,5},{8,11},{11,8},{9,1... | collective-permute-start | bytes 798728 | tf_op jit(solution)/shard_map/ppermute | solution.py:421
  13.4 19.3 %collective-permute-start.1 = (bf16[1024,128]{1,0:T(8,128)(2,1)}, bf16[1024,128]{1,0:T(8,128)(2,1)S(1)}, u32[]{:S(2)}, u32[]{:S(2)}) collective-permute-start(bf16[1024,128]{1,0:T(8,128)(2,1)} %get-tuple-element.40), channel_id=1, source_target_pairs={{0,1},{1,0},{2,3},{3,2},{4,5},{5,4},{6,7},{7,6},{8,9},{9,8},{10,11... | collective-permute-start | bytes 786440 | tf_op jit(solution)/shard_map/ppermute | solution.py:425
  13.7 25.5 %collective-permute-start.7 = (bf16[1040,128]{1,0:T(8,128)(2,1)}, bf16[1040,128]{1,0:T(8,128)(2,1)S(1)}, u32[]{:S(2)}, u32[]{:S(2)}) collective-permute-start(bf16[1040,128]{1,0:T(8,128)(2,1)} %get-tuple-element.50), channel_id=1, source_target_pairs={{0,1},{1,0},{2,3},{3,2},{4,5},{5,4},{6,7},{7,6},{8,9},{9,8},{10,11... | collective-permute-start | bytes 798728 | tf_op jit(solution)/shard_map/ppermute | solution.py:422
  14.9 26.4 %collective-permute-start.11 = (bf16[1040,128]{1,0:T(8,128)(2,1)}, bf16[1040,128]{1,0:T(8,128)(2,1)S(1)}, u32[]{:S(2)}, u32[]{:S(2)}) collective-permute-start(bf16[1040,128]{1,0:T(8,128)(2,1)} %get-tuple-element.57), channel_id=1, source_target_pairs={{0,3},{3,0},{1,2},{2,1},{4,7},{7,4},{5,6},{6,5},{8,11},{11,8},{9,1... | collective-permute-start | bytes 798728 | tf_op jit(solution)/shard_map/ppermute | solution.py:422
  20.5 2.1 %copy-start.10 = (bf16[1040,128]{1,0:T(8,128)(2,1)}, bf16[1040,128]{1,0:T(8,128)(2,1)S(1)}, u32[]{:S(2)}) copy-start(bf16[1040,128]{1,0:T(8,128)(2,1)S(1)} %get-tuple-element.59) | copy-start | bytes 798724
  20.5 21.4 %collective-permute-start.10 = (bf16[1040,128]{1,0:T(8,128)(2,1)}, bf16[1040,128]{1,0:T(8,128)(2,1)S(1)}, u32[]{:S(2)}, u32[]{:S(2)}) collective-permute-start(bf16[1040,128]{1,0:T(8,128)(2,1)} %get-tuple-element.56), channel_id=1, source_target_pairs={{0,3},{3,0},{1,2},{2,1},{4,7},{7,4},{5,6},{6,5},{8,11},{11,8},{9,1... | collective-permute-start | bytes 798728 | tf_op jit(solution)/shard_map/ppermute | solution.py:424
  22.6 14.0 %collective-permute-start.2 = (bf16[1024,128]{1,0:T(8,128)(2,1)}, bf16[1024,128]{1,0:T(8,128)(2,1)S(1)}, u32[]{:S(2)}, u32[]{:S(2)}) collective-permute-start(bf16[1024,128]{1,0:T(8,128)(2,1)} %get-tuple-element.42), channel_id=1, source_target_pairs={{0,3},{3,0},{1,2},{2,1},{4,7},{7,4},{5,6},{6,5},{8,11},{11,8},{9,1... | collective-permute-start | bytes 786440 | tf_op jit(solution)/shard_map/ppermute | solution.py:425
  24.1 59.9 %copy-start = (bf16[32,16,256]{2,1,0:T(8,128)(2,1)S(1)}, bf16[32,16,256]{2,1,0:T(8,128)(2,1)}, u32[]{:S(2)}) copy-start(bf16[32,16,256]{2,1,0:T(8,128)(2,1)} %param.16) | copy-start | bytes 786436
  24.1 59.9 %copy-start.4 = (bf16[8,256]{1,0:T(8,128)(2,1)S(1)}, bf16[8,256]{1,0:T(8,128)(2,1)}, u32[]{:S(2)}) copy-start(bf16[8,256]{1,0:T(8,128)(2,1)} %fresh.1) | copy-start | bytes 12292
  24.1 59.9 %copy-start.6 = (s32[8,4]{0,1:T(4,128)S(1)}, s32[8,4]{0,1:T(4,128)}, u32[]{:S(2)}) copy-start(s32[8,4]{0,1:T(4,128)} %param.17) | copy-start | bytes 388
  24.1 60.0 %copy-start.9 = (s32[8]{0:T(128)S(1)}, s32[8]{0:T(128)}, u32[]{:S(2)}) copy-start(s32[8]{0:T(128)} %param.18) | copy-start | bytes 100
  24.1 26.3 %all-to-all-start = ((bf16[16,8,1024]{2,1,0:T(8,128)(2,1)}), bf16[16,8,1024]{2,1,0:T(8,128)(2,1)S(1)}, u32[]{:S(2)}, u32[]{:S(2)}) async-start(bf16[16,8,1024]{2,1,0:T(8,128)(2,1)} %broadcast_in_dim.2), calls=%async_computation | async-start | bytes 524288 | tf_op jit(solution)/shard_map/all_to_all | solution.py:431
  32.8 9.5 %collective-permute-start.12 = (bf16[1040,128]{1,0:T(8,128)(2,1)}, bf16[1040,128]{1,0:T(8,128)(2,1)S(1)}, u32[]{:S(2)}, u32[]{:S(2)}) collective-permute-start(bf16[1040,128]{1,0:T(8,128)(2,1)} %copy-done.10), channel_id=1, source_target_pairs={{0,1},{1,0},{2,3},{3,2},{4,5},{5,4},{6,7},{7,6},{8,9},{9,8},{10,11... | collective-permute-start | bytes 798728 | tf_op jit(solution)/shard_map/ppermute | solution.py:424
  36.6 0.7 copy-start.1
  37.3 13.1 %collective-permute-start = (bf16[1024,128]{1,0:T(8,128)(2,1)}, bf16[1024,128]{1,0:T(8,128)(2,1)S(1)}, u32[]{:S(2)}, u32[]{:S(2)}) collective-permute-start(bf16[1024,128]{1,0:T(8,128)(2,1)} %get-tuple-element.38), channel_id=1, source_target_pairs={{0,1},{1,0},{2,3},{3,2},{4,5},{5,4},{6,7},{7,6},{8,9},{9,8},{10,11... | collective-permute-start | bytes 786440 | tf_op jit(solution)/shard_map/ppermute | solution.py:426
  37.3 1.0 copy-start.2
  39.2 14.5 %collective-permute-start.4 = (bf16[1024,128]{1,0:T(8,128)(2,1)}, bf16[1024,128]{1,0:T(8,128)(2,1)S(1)}, u32[]{:S(2)}, u32[]{:S(2)}) collective-permute-start(bf16[1024,128]{1,0:T(8,128)(2,1)} %get-tuple-element.45), channel_id=1, source_target_pairs={{0,3},{3,0},{1,2},{2,1},{4,7},{7,4},{5,6},{6,5},{8,11},{11,8},{9,1... | collective-permute-start | bytes 786440 | tf_op jit(solution)/shard_map/ppermute | solution.py:426
  41.3 12.4 %collective-permute-start.3 = (bf16[1024,128]{1,0:T(8,128)(2,1)}, bf16[1024,128]{1,0:T(8,128)(2,1)S(1)}, u32[]{:S(2)}, u32[]{:S(2)}) collective-permute-start(bf16[1024,128]{1,0:T(8,128)(2,1)} %get-tuple-element.44), channel_id=1, source_target_pairs={{0,3},{3,0},{1,2},{2,1},{4,7},{7,4},{5,6},{6,5},{8,11},{11,8},{9,1... | collective-permute-start | bytes 786440 | tf_op jit(solution)/shard_map/ppermute | solution.py:434
  41.9 11.9 %collective-permute-start.5 = (bf16[1024,128]{1,0:T(8,128)(2,1)}, bf16[1024,128]{1,0:T(8,128)(2,1)}, u32[]{:S(2)}, u32[]{:S(2)}) collective-permute-start(bf16[1024,128]{1,0:T(8,128)(2,1)} %get-tuple-element.47), channel_id=1, source_target_pairs={{0,1},{1,0},{2,3},{3,2},{4,5},{5,4},{6,7},{7,6},{8,9},{9,8},{10,11... | collective-permute-start | bytes 786440 | tf_op jit(solution)/shard_map/ppermute | solution.py:434
  43.3 18.6 %collective-permute-start.13 = (bf16[1040,128]{1,0:T(8,128)(2,1)}, bf16[1040,128]{1,0:T(8,128)(2,1)S(1)}, u32[]{:S(2)}, u32[]{:S(2)}) collective-permute-start(bf16[1040,128]{1,0:T(8,128)(2,1)} %get-tuple-element.60), channel_id=1, source_target_pairs={{0,4},{4,0},{1,5},{5,1},{2,6},{6,2},{3,7},{7,3},{8,12},{12,8},{9,1... | collective-permute-start | bytes 798728 | tf_op jit(solution)/shard_map/ppermute | solution.py:436
  50.4 11.0 %collective-permute-start.14 = (bf16[128,1024]{1,0:T(8,128)(2,1)S(1)}, bf16[128,1024]{1,0:T(8,128)(2,1)S(1)}, u32[]{:S(2)}, u32[]{:S(2)}) collective-permute-start(bf16[128,1024]{1,0:T(8,128)(2,1)S(1)} %bitcast.10), channel_id=1, source_target_pairs={{0,128},{128,0},{1,129},{129,1},{2,130},{130,2},{3,131},{131,3},{4... | collective-permute-start | bytes 786440 | tf_op jit(solution)/shard_map/ppermute | solution.py:432
  55.7 20.4 %collective-permute-start.6 = (bf16[1024,128]{1,0:T(8,128)(2,1)}, bf16[1024,128]{1,0:T(8,128)(2,1)S(1)}, u32[]{:S(2)}, u32[]{:S(2)}) collective-permute-start(bf16[1024,128]{1,0:T(8,128)(2,1)} %get-tuple-element.48), channel_id=1, source_target_pairs={{0,4},{4,0},{1,5},{5,1},{2,6},{6,2},{3,7},{7,3},{8,12},{12,8},{9,1... | collective-permute-start | bytes 786440 | tf_op jit(solution)/shard_map/ppermute | solution.py:438
  77.4 18.8 %all-to-all-start.1 = ((bf16[32,8,640]{2,1,0:T(8,128)(2,1)}), bf16[32,8,640]{2,1,0:T(8,128)(2,1)S(1)}, u32[]{:S(2)}, u32[]{:S(2)}) async-start(bf16[32,8,640]{2,1,0:T(8,128)(2,1)} %bitcast.4), calls=%async_computation.1 | async-start | bytes 655360 | tf_op jit(solution)/shard_map/all_to_all | solution.py:455
